TPU v7x, 32 devices: a whole 2x2x4 slice. The times are simulated.
32 devices in a mesh: grp: 2 (over x), gx: 8 (over z, y), gy: 2 (over core).
Axes of the slice: x: 2, y: 2, z: 4, core: 2. Of those that a mesh axis runs over, the one named last changes fastest.
Arguments:
- warmth_anomaly: float32 [64, 128, 256], P('grp', 'gx', 'gy'), may hold values from -6 to 6
- humidity_anomaly: float32 [64, 128, 256], P('grp', 'gx', 'gy'), may hold values from -6 to 6
- horizontal_line_advective_ratio: float32 [64], replicated, may hold values from -0.5 to 0.5
- vertical_line_advective_ratio: float32 [64], replicated, may hold values from -0.5 to 0.5
- molecular_extinction_coefficient: float32 [112], replicated, may hold values from 0.002 to 0.05
- droplet_extinction_thickness: float32 [112], replicated, may hold values from 0.005 to 0.1
- shortwave_quadrature_share: float32 [112], replicated, may hold values from 0.5 to 5
- longwave_quadrature_share: float32 [112], replicated, may hold values from 0.5 to 5
- overcast_layer_flags: int32 [8192, 64], P(('grp', 'gx', 'gy')), may hold values 0 or 1
- profile_position_within_tile: int32 [64, 128], P('gx', 'gy'), may hold values from 0 to 511, as said below
Outputs:
- temperature_out: float32 [64, 128, 256], P('grp', 'gx', 'gy')
- moisture_out: float32 [64, 128, 256], P('grp', 'gx', 'gy')
- warming_rates: float32 [8192, 64], P(('grp', 'gx', 'gy'))
Inputs may be any that keep to these rules, and one draw needn't show every extreme that they name: `profile_position_within_tile`: each tile's block of 8 x 64 entries holds every number from 0 to 511 exactly once.
All inputs are finite; a program needn't handle non-finite values. No bound on the sum of `overcast_layer_flags` on one device may be relied on, other than what follows from the above.
Results may differ from a plain program's by a relative error of at most 0.000092.
Values sent between devices are 32-bit elements; how exact they have to be, the bound alone decides.
A program may use at most 64 MiB of HBM per device.

v0:
```python
import functools
import math

import jax
import jax.numpy as jnp
from jax import lax
from jax.experimental import pallas as pl
from jax.experimental.pallas import tpu as pltpu
from jax.sharding import PartitionSpec as P

SWEEPS = 8
NU_H = 0.15
NU_V = 0.15
HEATING_INTERVAL = 0.5
M = 8
MESH = pl.DeviceIdType.MESH
BF = jnp.bfloat16
F32 = jnp.float32


def split_bf16(x):
    hi = x.astype(BF)
    lo = (x - hi.astype(F32)).astype(BF)
    return hi, lo


def kernel(
    n_gx, n_gy, L, R, C, S, B, G,
    warm_in, humid_in, cx_ref, cy_ref, gas_ref, drop_ref, sw_ref, lw_ref, flags_ref, slot_ref,
    t_out, m_out, rates_out,
    ext, edge_send, edge_recv, qt, packed, rad, coef, cloudy, absorber, theta, rates, heat, ucols,
    hedge_send, hedge_recv, rows_send, rows_recv,
    halo_send_sem, halo_recv_sem, edge_send_sem, edge_recv_sem, misc_send_sem, misc_recv_sem,
):
    g = lax.axis_index("grp")
    x = lax.axis_index("gx")
    y = lax.axis_index("gy")
    og = 1 - g
    xn, xp = lax.rem(x + 1, n_gx), lax.rem(x + n_gx - 1, n_gx)
    yn, yp = lax.rem(y + 1, n_gy), lax.rem(y + n_gy - 1, n_gy)
    fields = (warm_in, humid_in)
    outs = (t_out, m_out)
    LE = L + M
    T = (R + 2 * M) // 8
    per = C // T
    NP = -(-LE // per)
    RI = R // 2
    RLO = 8
    ROWN = RLO + M
    RE = R + 2 * M

    barrier = pltpu.get_barrier_semaphore()
    for dev in ((g, xn, y), (g, xp, y), (og, x, y), (og, xn, y), (og, xp, y), (g, x, yn), (g, x, yp)):
        pl.semaphore_signal(barrier, inc=1, device_id=dev, device_id_type=MESH)
    pl.semaphore_wait(barrier, 7)

    def remote(src, dst, ss, rs, dev):
        c = pltpu.make_async_remote_copy(
            src_ref=src, dst_ref=dst, send_sem=ss, recv_sem=rs, device_id=dev, device_id_type=MESH
        )
        c.start()
        return c

    half = slot_ref.shape[1]
    slots = slot_ref[...]
    rep = (
        lax.broadcasted_iota(jnp.int32, (half, C), 1) // 2
        == lax.broadcasted_iota(jnp.int32, (half, C), 0)
    ).astype(F32).astype(BF)
    s_hi = (slots // 16).astype(F32).astype(BF)
    s_lo = (slots % 16).astype(F32).astype(BF)
    slot_rep = (
        16.0 * jnp.dot(s_hi, rep, preferred_element_type=F32)
        + jnp.dot(s_lo, rep, preferred_element_type=F32)
    ).astype(jnp.int32)
    s_iota = lax.broadcasted_iota(jnp.int32, (S, C), 0)
    for i in range(RI):
        qt[:, i * C : (i + 1) * C] = jnp.where(s_iota == slot_rep[i : i + 1, :], 1.0, 0.0).astype(BF)
    parts = []
    for i in range(RI):
        col = []
        for f in range(2):
            flat = fields[f].reshape(L * R, C)
            col.append(
                flat[pl.ds(2 * i, L, stride=R), :] + flat[pl.ds(2 * i + 1, L, stride=R), :]
            )
        hi, lo = split_bf16(0.25 * jnp.concatenate(col, axis=0))
        parts.append(jnp.concatenate([hi, lo], axis=0))
    lhs = jnp.concatenate(parts, axis=1)
    both = lax.dot_general(
        lhs, qt[...], (((1,), (1,)), ((), ())), preferred_element_type=F32
    )
    both = both[: 2 * L] + both[2 * L :]
    for h in range(2):
        packed[h] = both[:, h * B : (h + 1) * B]
    c_packed = remote(packed.at[og], rad.at[g], misc_send_sem.at[0], misc_recv_sem.at[0], (og, x, y))

    lev_src = (L - M) * og
    lev_dst = 1 + L * g
    own_dst = 1 + M * g
    halos = []
    n = 0
    for f in range(2):
        for levs, dlevs, count, gg in ((0, own_dst, L, g), (lev_src, lev_dst, M, og)):
            for r0, d0, xx in ((R - M, RLO, xn), (0, ROWN + R, xp)):
                halos.append(remote(
                    fields[f].at[pl.ds(levs, count), r0 : r0 + M, :],
                    ext.at[0, f, pl.ds(dlevs, count), d0 : d0 + M, :],
                    halo_send_sem.at[n], halo_recv_sem.at[n], (gg, xx, y),
                ))
                n += 1
        halos.append(remote(
            fields[f].at[pl.ds(lev_src, M)],
            ext.at[0, f, pl.ds(lev_dst, M), ROWN : ROWN + R, :],
            halo_send_sem.at[n], halo_recv_sem.at[n], (og, x, y),
        ))
        n += 1
    rad[g] = packed[g]
    for f in range(2):
        ext[0, f, pl.ds(own_dst, L), ROWN : ROWN + R, :] = fields[f][...]
        for b in range(2):
            for p in (0, LE + 1):
                ext[b, f, p] = jnp.zeros_like(ext[b, f, p])

    log2e = 1.0 / math.log(2.0)
    for q, (ref, scale) in enumerate(((gas_ref, -log2e), (drop_ref, -log2e), (sw_ref, 1.0), (lw_ref, 1.0))):
        coef[q] = jnp.broadcast_to(ref[...] * scale, (128, G)).T
    for hb in range(B // 128):
        cloudy[hb] = flags_ref[hb * 128 : (hb + 1) * 128, :].astype(F32).T

    c_packed.wait()
    for o in range(2):
        mo = rad[o, L : 2 * L, :]
        soft = jnp.maximum(mo, 0.0) + jnp.log1p(jnp.exp(-jnp.abs(mo)))
        for hb in range(B // 128):
            absorber[hb, o * L : (o + 1) * L, :] = soft[:, hb * 128 : (hb + 1) * 128]
            theta[hb, o * L : (o + 1) * L, :] = rad[o, 0:L, hb * 128 : (hb + 1) * 128]

    GB = G // 8
    norm = 4.0 / G
    for hb in range(B // 128):
        for o in range(2):
            def level(l, flux, o=o, hb=hb):
                lg = l + o * L
                a = jnp.broadcast_to(absorber[hb, pl.ds(lg, 1), :], (8, 128))
                c = jnp.broadcast_to(cloudy[hb, pl.ds(lg, 1), :], (8, 128))
                th = 1.0 + 0.1 * theta[hb, pl.ds(lg, 1), :]
                sw = lw = None
                new = []
                for q in range(GB):
                    rows = slice(8 * q, 8 * q + 8)
                    d = 1.0 - jnp.exp2(a * coef[0, rows, :] + c * coef[1, rows, :])
                    s = flux[q] * d
                    w = coef[3, rows, :] * d
                    sw = s if sw is None else sw + s
                    lw = w if lw is None else lw + w
                    new.append(flux[q] - s)
                total = jnp.sum(sw - lw * th, axis=0, keepdims=True) * norm
                rates[o, hb, pl.ds(l, 1), :] = total
                return tuple(new)

            if o == 0:
                flux = tuple(coef[2, 8 * q : 8 * q + 8, :] for q in range(GB))
            flux = lax.fori_loop(0, L, level, flux, unroll=2)
    c_heat = remote(rates.at[og], heat.at[g], misc_send_sem.at[1], misc_recv_sem.at[1], (og, x, y))
    heat[g] = rates[g]
    for o in range(2):
        for hb in range(B // 128):
            rates_out[hb * 128 : (hb + 1) * 128, o * L : (o + 1) * L] = rates[o, hb].T

    lane = lax.broadcasted_iota(jnp.int32, (8, C), 1)

    def pack(vals, j, accs):
        right, left = accs
        for t in range(T):
            k = j * T + t
            turned = pltpu.roll(vals[8 * t : 8 * t + 8, :], lax.rem(k + 1, C), 1)
            right = jnp.where(lane == k, turned, right)
            left = jnp.where(lane == lax.rem(k + 1, C), turned, left)
        return right, left

    def send_edges(k, f):
        return (
            remote(edge_send.at[k, f, 0], edge_recv.at[k, f, 0],
                   edge_send_sem.at[k, f, 0], edge_recv_sem.at[k, f, 0], (g, x, yn)),
            remote(edge_send.at[k, f, 1], edge_recv.at[k, f, 1],
                   edge_send_sem.at[k, f, 1], edge_recv_sem.at[k, f, 1], (g, x, yp)),
        )

    zero = jnp.zeros((8, C), F32)

    def run_levels(k, f, count, values):
        for p in range(NP):
            lo, hi = p * per, min(count, (p + 1) * per)
            if lo >= hi:
                edge_send[k, f, 0, p] = zero
                edge_send[k, f, 1, p] = zero
                continue
            right, left = lax.fori_loop(
                lo, hi, lambda j, accs, lo=lo: pack(values(j), j - lo, accs), (zero, zero), unroll=2
            )
            edge_send[k, f, 0, p] = right
            edge_send[k, f, 1, p] = left

    def first(f):
        run_levels(0, f, LE, lambda j: ext[0, f, j + 1, RLO : RLO + RE, :])
        return send_edges(0, f)

    def sweep(k, f):
        src, dst = (k - 1) % 2, k % 2
        start = g * k
        last = k == SWEEPS
        t0, t1 = (M // 8, M // 8 + R // 8) if last else (0, T)
        r0, r1 = RLO + 8 * t0, RLO + 8 * t1

        def values(j):
            lev = start + j
            p = lev + 1
            jj = j + g
            which = jj // per
            kk = (jj - which * per) * T
            from_left = edge_recv[k - 1, f, 0, which]
            from_right = edge_recv[k - 1, f, 1, which]
            lg = lev + (L - M) * g
            sx = 0.5 * cx_ref[lg]
            sy = 0.5 * cy_ref[lg]
            cen = ext[src, f, p, r0:r1, :]
            base = (
                (1.0 - 4.0 * NU_H - 2.0 * NU_V) * cen
                + NU_V * (ext[src, f, p + 1, r0:r1, :] + ext[src, f, p - 1, r0:r1, :])
                + (NU_H - sx) * ext[src, f, p, r0 + 1 : r1 + 1, :]
                + (NU_H + sx) * ext[src, f, p, r0 - 1 : r1 - 1, :]
            )
            res = []
            for t in range(t0, t1):
                q = 8 * (t - t0)
                v = cen[q : q + 8, :]
                kt = kk + t
                prev = jnp.where(lane == 0, pltpu.roll(from_left, lax.rem(C - kt, C), 1), pltpu.roll(v, 1, 1))
                nxt = jnp.where(
                    lane == C - 1, pltpu.roll(from_right, lax.rem(2 * C - 2 - kt, C), 1), pltpu.roll(v, C - 1, 1)
                )
                res.append(base[q : q + 8, :] + (NU_H - sy) * nxt + (NU_H + sy) * prev)
            new = jnp.concatenate(res, axis=0)
            if last:
                outs[f][j] = new
            else:
                ext[dst, f, p, RLO : RLO + RE, :] = new
            return new

        count = LE - k
        if last:
            @pl.loop(0, count, unroll=2)
            def _(j):
                values(j)
            return None
        run_levels(k, f, count, values)
        return send_edges(k, f)

    for c in halos:
        c.wait()
    flight = [first(0), first(1)]
    sent = []

    def advance(ks):
        for k in ks:
            for f in range(2):
                for c in flight[f]:
                    c.wait()
                flight[f] = sweep(k, f)

    advance((1, 2))

    c_heat.wait()
    hi, lo = split_bf16(jnp.concatenate([heat[h, hb] for h in range(2) for hb in range(B // 128)], axis=1))
    spread = jnp.dot(jnp.concatenate([hi, lo], axis=0), qt[...], preferred_element_type=F32)
    spread = spread[:L] + spread[L:]
    LT = L // 8
    ehi = zero
    elo = zero
    for i in range(RI):
        ui = spread[:, i * C : (i + 1) * C]
        ucols[i] = ui
        for t in range(LT):
            k = i * LT + t
            turned = pltpu.roll(ui[8 * t : 8 * t + 8, :], (k + 1) % C, 1)
            ehi = jnp.where(lane == k, turned, ehi)
            elo = jnp.where(lane == (k + 1) % C, turned, elo)
    hedge_send[0] = ehi
    hedge_send[1] = elo
    c_he = [
        remote(hedge_send.at[0], hedge_recv.at[0], misc_send_sem.at[2], misc_recv_sem.at[2], (g, x, yn)),
        remote(hedge_send.at[1], hedge_recv.at[1], misc_send_sem.at[3], misc_recv_sem.at[3], (g, x, yp)),
    ]
    advance((3,))
    for c in c_he:
        c.wait()
    from_left = hedge_recv[0]
    from_right = hedge_recv[1]
    even = lane % 2 == 0
    for i in range(RI):
        for t in range(LT):
            k = i * LT + t
            v = ucols[i, 8 * t : 8 * t + 8, :]
            prev = jnp.where(lane == 0, pltpu.roll(from_left, (C - k) % C, 1), pltpu.roll(v, 1, 1))
            nxt = jnp.where(lane == C - 1, pltpu.roll(from_right, (2 * C - 2 - k) % C, 1), pltpu.roll(v, C - 1, 1))
            w = 0.75 * v + 0.25 * jnp.where(even, prev, nxt)
            ucols[i, 8 * t : 8 * t + 8, :] = w
            if i == 0:
                rows_send[0, 8 * t : 8 * t + 8, :] = w
            if i == RI - 1:
                rows_send[1, 8 * t : 8 * t + 8, :] = w
    c_rows = [
        remote(rows_send.at[0], rows_recv.at[0], misc_send_sem.at[4], misc_recv_sem.at[4], (g, xp, y)),
        remote(rows_send.at[1], rows_recv.at[1], misc_send_sem.at[5], misc_recv_sem.at[5], (g, xn, y)),
    ]
    advance(range(4, SWEEPS + 1))
    for c in c_rows:
        c.wait()
    flat = t_out.reshape(L * R, C)
    for i in range(RI):
        v = ucols[i]
        above = rows_recv[1] if i == 0 else ucols[i - 1]
        below = rows_recv[0] if i == RI - 1 else ucols[i + 1]
        flat[pl.ds(2 * i, L, stride=R), :] = flat[pl.ds(2 * i, L, stride=R), :] + HEATING_INTERVAL * (0.75 * v + 0.25 * above)
        flat[pl.ds(2 * i + 1, L, stride=R), :] = flat[pl.ds(2 * i + 1, L, stride=R), :] + HEATING_INTERVAL * (0.75 * v + 0.25 * below)


def body(n_gx, n_gy, warm, humid, cx, cy, gas, drop, sw, lw, flags, slots):
    L, R, C = warm.shape
    S = slots.shape[0] * slots.shape[1]
    B = flags.shape[0]
    G = gas.shape[0]
    LE = L + M
    T = (R + 2 * M) // 8
    NP = -(-LE // (C // T))
    vmem = pl.BlockSpec(memory_space=pltpu.VMEM)
    smem = pl.BlockSpec(memory_space=pltpu.SMEM)
    return pl.pallas_call(
        functools.partial(kernel, n_gx, n_gy, L, R, C, S, B, G),
        out_shape=(
            jax.ShapeDtypeStruct((L, R, C), F32),
            jax.ShapeDtypeStruct((L, R, C), F32),
            jax.ShapeDtypeStruct((B, 2 * L), F32),
        ),
        in_specs=[vmem, vmem, smem, smem] + [vmem] * 6,
        out_specs=(vmem, vmem, vmem),
        scratch_shapes=[
            pltpu.VMEM((2, 2, LE + 2, R + 2 * M + 16, C), F32),
            pltpu.VMEM((SWEEPS, 2, 2, NP, 8, C), F32),
            pltpu.VMEM((SWEEPS, 2, 2, NP, 8, C), F32),
            pltpu.VMEM((S, (R // 2) * C), BF),
            pltpu.VMEM((2, 2 * L, B), F32),
            pltpu.VMEM((2, 2 * L, B), F32),
            pltpu.VMEM((4, G, 128), F32),
            pltpu.VMEM((B // 128, 2 * L, 128), F32),
            pltpu.VMEM((B // 128, 2 * L, 128), F32),
            pltpu.VMEM((B // 128, 2 * L, 128), F32),
            pltpu.VMEM((2, B // 128, L, 128), F32),
            pltpu.VMEM((2, B // 128, L, 128), F32),
            pltpu.VMEM((R // 2, L, C), F32),
            pltpu.VMEM((2, 8, C), F32),
            pltpu.VMEM((2, 8, C), F32),
            pltpu.VMEM((2, L, C), F32),
            pltpu.VMEM((2, L, C), F32),
            pltpu.SemaphoreType.DMA((10,)),
            pltpu.SemaphoreType.DMA((10,)),
            pltpu.SemaphoreType.DMA((SWEEPS, 2, 2)),
            pltpu.SemaphoreType.DMA((SWEEPS, 2, 2)),
            pltpu.SemaphoreType.DMA((6,)),
            pltpu.SemaphoreType.DMA((6,)),
        ],
        compiler_params=pltpu.CompilerParams(collective_id=0, has_side_effects=True),
    )(
        warm, humid, cx, cy, gas[None], drop[None], sw[None], lw[None], flags, slots,
    )


def solution(mesh):
    assert mesh.shape["grp"] == 2
    in_specs = (
        P("grp", "gx", "gy"), P("grp", "gx", "gy"), P(), P(), P(), P(), P(), P(),
        P(("grp", "gx", "gy"), None), P("gx", "gy"),
    )
    out_specs = (P("grp", "gx", "gy"), P("grp", "gx", "gy"), P(("grp", "gx", "gy"), None))
    return jax.shard_map(
        functools.partial(body, mesh.shape["gx"], mesh.shape["gy"]),
        mesh=mesh, in_specs=in_specs, out_specs=out_specs, check_vma=False,
    )
```

profile of v0, /device:TPU:0, one launch (start us, length us, event | category | flops | bytes accessed | tf_op | source)
XLA Modules:
  0.0 84.3 jit_solution(2991885656773332034)
XLA Ops:
  0.6 1.6 %copy.13.flags_ref = s32[256,64]{1,0:T(8,128)} copy(s32[256,64]{0,1:T(8,128)} %param.18) | data formatting | bytes 131072 | tf_op args[8]
  2.2 78.0 %shard_map.121 = (f32[32,16,128]{2,1,0:T(8,128)}, f32[32,16,128]{2,1,0:T(8,128)}, f32[256,64]{1,0:T(8,128)}) custom-call(f32[32,16,128]{2,1,0:T(8,128)} %warm_in.1, f32[32,16,128]{2,1,0:T(8,128)} %humid_in.1, f32[64]{0:T(128)} %cx_ref.1, f32[64]{0:T(128)} %cy_ref.1, f32[1,112]{1,0:T(1,128)} %bitcast.4, f32[1,112]{1,0:T(1,128)} %bitcast.5, f32[1,112]{1,0:T(1,128)} %bitcast.6, ...), custom_call_target="tpu_custom_call" | custom-call | tf_op jit(solution)/shard_map/pallas_call | solution.py:339
  80.3 1.6 %copy.14 = f32[256,64]{0,1:T(8,128)} copy(f32[256,64]{1,0:T(8,128)} %get-tuple-element.5) | data formatting | bytes 131072 | tf_op jit(solution)/shard_map/pallas_call | solution.py:339
  81.9 0.0 copy-start
  81.9 1.7 %copy.17 = f32[32,16,128]{2,1,0:T(8,128)} copy(f32[32,16,128]{2,1,0:T(8,128)} %get-tuple-element.9) | data formatting | bytes 524288
  83.6 0.0 copy-done
  83.6 0.7 copy.18
Async XLA Ops:
  81.9 1.7 %copy-start = (f32[32,16,128]{2,1,0:T(8,128)S(1)}, f32[32,16,128]{2,1,0:T(8,128)}, u32[]{:S(2)}) copy-start(f32[32,16,128]{2,1,0:T(8,128)} %get-tuple-element.10) | copy-start | bytes 786436
where the time goes:
time: 84.5 us; the launch traced here: 84.3 us
  Pallas kernels  78 us (92%)
  local copies, waits for them, and re-layouts  5.63 us (7%)
    pallas_call x1, Pallas kernels, body(): pl.pallas_call(functools.partial(kernel, n_gx, n_gy, L, R, C, S, B, G), o...  78 us
    unnamed x5, local copies, waits for them, and re-layouts  4.01 us

commit v1 on v0

--- a/solution.py
+++ b/solution.py
@@ -12,6 +12,7 @@
 NU_H = 0.15
 NU_V = 0.15
 HEATING_INTERVAL = 0.5
+UNROLL = 8
 M = 8
 MESH = pl.DeviceIdType.MESH
 BF = jnp.bfloat16
@@ -28,7 +29,7 @@
     n_gx, n_gy, L, R, C, S, B, G,
     warm_in, humid_in, cx_ref, cy_ref, gas_ref, drop_ref, sw_ref, lw_ref, flags_ref, slot_ref,
     t_out, m_out, rates_out,
-    ext, edge_send, edge_recv, qt, packed, rad, coef, cloudy, absorber, theta, rates, heat, ucols,
+    ext0, ext1, edge_send, edge_recv, qt, packed, rad, coef, cloudy, absorber, theta, rates, heat, ucols,
     hedge_send, hedge_recv, rows_send, rows_recv,
     halo_send_sem, halo_recv_sem, edge_send_sem, edge_recv_sem, misc_send_sem, misc_recv_sem,
 ):
@@ -39,6 +40,7 @@
     xn, xp = lax.rem(x + 1, n_gx), lax.rem(x + n_gx - 1, n_gx)
     yn, yp = lax.rem(y + 1, n_gy), lax.rem(y + n_gy - 1, n_gy)
     fields = (warm_in, humid_in)
+    ext = (ext0, ext1)
     outs = (t_out, m_out)
     LE = L + M
     T = (R + 2 * M) // 8
@@ -105,28 +107,28 @@
             for r0, d0, xx in ((R - M, RLO, xn), (0, ROWN + R, xp)):
                 halos.append(remote(
                     fields[f].at[pl.ds(levs, count), r0 : r0 + M, :],
-                    ext.at[0, f, pl.ds(dlevs, count), d0 : d0 + M, :],
+                    ext0.at[f, pl.ds(dlevs, count), d0 : d0 + M, :],
                     halo_send_sem.at[n], halo_recv_sem.at[n], (gg, xx, y),
                 ))
                 n += 1
         halos.append(remote(
             fields[f].at[pl.ds(lev_src, M)],
-            ext.at[0, f, pl.ds(lev_dst, M), ROWN : ROWN + R, :],
+            ext0.at[f, pl.ds(lev_dst, M), ROWN : ROWN + R, :],
             halo_send_sem.at[n], halo_recv_sem.at[n], (og, x, y),
         ))
         n += 1
     rad[g] = packed[g]
     for f in range(2):
-        ext[0, f, pl.ds(own_dst, L), ROWN : ROWN + R, :] = fields[f][...]
+        ext0[f, pl.ds(own_dst, L), ROWN : ROWN + R, :] = fields[f][...]
         for b in range(2):
             for p in (0, LE + 1):
-                ext[b, f, p] = jnp.zeros_like(ext[b, f, p])
+                ext[b][f, p] = jnp.zeros((RE + 16, C), F32)
 
     log2e = 1.0 / math.log(2.0)
     for q, (ref, scale) in enumerate(((gas_ref, -log2e), (drop_ref, -log2e), (sw_ref, 1.0), (lw_ref, 1.0))):
         coef[q] = jnp.broadcast_to(ref[...] * scale, (128, G)).T
     for hb in range(B // 128):
-        cloudy[hb] = flags_ref[hb * 128 : (hb + 1) * 128, :].astype(F32).T
+        cloudy[hb] = flags_ref[:, hb * 128 : (hb + 1) * 128].astype(F32)
 
     c_packed.wait()
     for o in range(2):
@@ -166,7 +168,7 @@
     heat[g] = rates[g]
     for o in range(2):
         for hb in range(B // 128):
-            rates_out[hb * 128 : (hb + 1) * 128, o * L : (o + 1) * L] = rates[o, hb].T
+            rates_out[o * L : (o + 1) * L, hb * 128 : (hb + 1) * 128] = rates[o, hb]
 
     lane = lax.broadcasted_iota(jnp.int32, (8, C), 1)
 
@@ -197,13 +199,14 @@
                 edge_send[k, f, 1, p] = zero
                 continue
             right, left = lax.fori_loop(
-                lo, hi, lambda j, accs, lo=lo: pack(values(j), j - lo, accs), (zero, zero), unroll=2
+                lo, hi, lambda j, accs, lo=lo: pack(values(j), j - lo, accs), (zero, zero),
+                unroll=min(UNROLL, hi - lo),
             )
             edge_send[k, f, 0, p] = right
             edge_send[k, f, 1, p] = left
 
     def first(f):
-        run_levels(0, f, LE, lambda j: ext[0, f, j + 1, RLO : RLO + RE, :])
+        run_levels(0, f, LE, lambda j: ext0[f, j + 1, RLO : RLO + RE, :])
         return send_edges(0, f)
 
     def sweep(k, f):
@@ -224,12 +227,12 @@
             lg = lev + (L - M) * g
             sx = 0.5 * cx_ref[lg]
             sy = 0.5 * cy_ref[lg]
-            cen = ext[src, f, p, r0:r1, :]
+            cen = ext[src][f, p, r0:r1, :]
             base = (
                 (1.0 - 4.0 * NU_H - 2.0 * NU_V) * cen
-                + NU_V * (ext[src, f, p + 1, r0:r1, :] + ext[src, f, p - 1, r0:r1, :])
-                + (NU_H - sx) * ext[src, f, p, r0 + 1 : r1 + 1, :]
-                + (NU_H + sx) * ext[src, f, p, r0 - 1 : r1 - 1, :]
+                + NU_V * (ext[src][f, p + 1, r0:r1, :] + ext[src][f, p - 1, r0:r1, :])
+                + (NU_H - sx) * ext[src][f, p, r0 + 1 : r1 + 1, :]
+                + (NU_H + sx) * ext[src][f, p, r0 - 1 : r1 - 1, :]
             )
             res = []
             for t in range(t0, t1):
@@ -245,12 +248,12 @@
             if last:
                 outs[f][j] = new
             else:
-                ext[dst, f, p, RLO : RLO + RE, :] = new
+                ext[dst][f, p, RLO : RLO + RE, :] = new
             return new
 
         count = LE - k
         if last:
-            @pl.loop(0, count, unroll=2)
+            @pl.loop(0, count, unroll=UNROLL)
             def _(j):
                 values(j)
             return None
@@ -326,27 +329,35 @@
         flat[pl.ds(2 * i + 1, L, stride=R), :] = flat[pl.ds(2 * i + 1, L, stride=R), :] + HEATING_INTERVAL * (0.75 * v + 0.25 * below)
 
 
+def hand_on(t_in, m_in, r_in, t_out, m_out, r_out):
+    t_out[...] = t_in[...]
+    m_out[...] = m_in[...]
+    r_out[...] = r_in[...]
+
+
 def body(n_gx, n_gy, warm, humid, cx, cy, gas, drop, sw, lw, flags, slots):
     L, R, C = warm.shape
     S = slots.shape[0] * slots.shape[1]
     B = flags.shape[0]
+    flags = flags.T
     G = gas.shape[0]
     LE = L + M
     T = (R + 2 * M) // 8
     NP = -(-LE // (C // T))
     vmem = pl.BlockSpec(memory_space=pltpu.VMEM)
     smem = pl.BlockSpec(memory_space=pltpu.SMEM)
-    return pl.pallas_call(
+    t, m, rates = pl.pallas_call(
         functools.partial(kernel, n_gx, n_gy, L, R, C, S, B, G),
         out_shape=(
             jax.ShapeDtypeStruct((L, R, C), F32),
             jax.ShapeDtypeStruct((L, R, C), F32),
-            jax.ShapeDtypeStruct((B, 2 * L), F32),
+            jax.ShapeDtypeStruct((2 * L, B), F32),
         ),
         in_specs=[vmem, vmem, smem, smem] + [vmem] * 6,
         out_specs=(vmem, vmem, vmem),
         scratch_shapes=[
-            pltpu.VMEM((2, 2, LE + 2, R + 2 * M + 16, C), F32),
+            pltpu.VMEM((2, LE + 2, R + 2 * M + 16, C), F32),
+            pltpu.VMEM((2, LE + 2, R + 2 * M + 16, C), F32),
             pltpu.VMEM((SWEEPS, 2, 2, NP, 8, C), F32),
             pltpu.VMEM((SWEEPS, 2, 2, NP, 8, C), F32),
             pltpu.VMEM((S, (R // 2) * C), BF),
@@ -374,6 +385,13 @@
     )(
         warm, humid, cx, cy, gas[None], drop[None], sw[None], lw[None], flags, slots,
     )
+    t, m, rates = pl.pallas_call(
+        hand_on,
+        out_shape=tuple(jax.ShapeDtypeStruct(a.shape, F32) for a in (t, m, rates)),
+        in_specs=[vmem] * 3,
+        out_specs=(vmem,) * 3,
+    )(t, m, rates)
+    return t, m, rates.T
 
 
 def solution(mesh):

time: 84.5 us -> 55.1 us (0.65)
  Pallas kernels: 78 us -> 54.3 us
  local copies, waits for them, and re-layouts: 5.63 us -> 0 us
    pallas_call x1, Pallas kernels: 78 us -> 52.4 us  [body(): pl.pallas_call(functools.partial(kernel, n_gx, n_gy, L, R, C, S, B, G), o...]
    unnamed x5 -> x0, local copies, waits for them, and re-layouts: 4.01 us -> none
    pallas_call x0 -> x1, Pallas kernels: none -> 1.85 us  [body(): pl.pallas_call(hand_on, out_shape=tuple((jax.ShapeDtypeStruct(a.shape, F3...]
    pallas_call x1 -> x0, local copies, waits for them, and re-layouts: 1.62 us -> none  [body(): pl.pallas_call(functools.partial(kernel, n_gx, n_gy, L, R, C, S, B, G), o...]
where the time goes in v1:
time: 55.1 us; the launch traced here: 54.9 us
  Pallas kernels  54.3 us (99%)
  between operations  0.64 us (1%)
    pallas_call x1, Pallas kernels, body(): pl.pallas_call(functools.partial(kernel, n_gx, n_gy, L, R, C, S, B, G), o...  52.4 us
    pallas_call x1, Pallas kernels, body(): pl.pallas_call(hand_on, out_shape=tuple((jax.ShapeDtypeStruct(a.shape, F3...  1.85 us

profile of v1, /device:TPU:0, one launch (start us, length us, event | category | flops | bytes accessed | tf_op | source)
XLA Modules:
  0.0 54.9 jit_solution(10352619479121035726)
XLA Ops:
  0.6 52.4 %shard_map.121 = (f32[32,16,128]{2,1,0:T(8,128)}, f32[32,16,128]{2,1,0:T(8,128)}, f32[64,256]{1,0:T(8,128)}) custom-call(f32[32,16,128]{2,1,0:T(8,128)} %warm_in.1, f32[32,16,128]{2,1,0:T(8,128)} %humid_in.1, f32[64]{0:T(128)} %cx_ref.1, f32[64]{0:T(128)} %cy_ref.1, f32[1,112]{1,0:T(1,128)} %bitcast.7, f32[1,112]{1,0:T(1,128)} %bitcast.8, f32[1,112]{1,0:T(1,128)} %bitcast.9, ...), custom_call_target="tpu_custom_call" | custom-call | tf_op jit(solution)/shard_map/pallas_call | solution.py:349
  53.1 1.9 %shard_map.122 = (f32[32,16,128]{2,1,0:T(8,128)}, f32[32,16,128]{2,1,0:T(8,128)}, f32[64,256]{1,0:T(8,128)}) custom-call(f32[32,16,128]{2,1,0:T(8,128)} %get-tuple-element.9.t_in, f32[32,16,128]{2,1,0:T(8,128)} %get-tuple-element.10.m_in, f32[64,256]{1,0:T(8,128)} %get-tuple-element.11.r_in), custom_call_target="tpu_custom_call" | custom-call | tf_op jit(solution)/shard_map/pallas_call | solution.py:388
